TPU v7x, 32 devices: a whole 2x2x4 slice. The times are simulated.
32 devices in a mesh: prow: 8 (over z, y), pcol: 4 (over x, core).
Axes of the slice: x: 2, y: 2, z: 4, core: 2. Of those that a mesh axis runs over, the one named last changes fastest.
Arguments:
- iface_tiles: int32 [32, 16], replicated, may hold values from 0 to 63, as said below
- interior_sizes: int32 [32], P(('prow', 'pcol')), may hold values from 128 to 512
- coupling: float32 [32, 512, 2048], P(('prow', 'pcol')), may hold values from -0.25 to 0.25
- factor_inverse: float32 [32, 512, 512], P(('prow', 'pcol')), as said below
- interface_block: float32 [8, 8, 4, 16, 128, 128], P('prow', None, 'pcol'), as said below
Outputs:
- schur: float32 [8, 8, 4, 16, 128, 128], P('prow', None, 'pcol')
- panel: float32 [8, 8, 128, 128], P('prow', None, 'pcol')
Inputs may be any that keep to these rules, and one draw needn't show every extreme that they name: `iface_tiles`: each row holds 16 distinct tile numbers; for every r, exactly 2 of them are r modulo 8; every tile number stands in exactly 8 rows. `factor_inverse`: each matrix is lower triangular with a diagonal between 0.25 and 1. `interface_block`: diagonal entries lie between 80 and 160; other entries are of order one.
All inputs are finite; a program needn't handle non-finite values.
Results may differ from a plain program's by a relative error of at most 0.0001.
Values sent between devices are 32-bit elements; how exact they have to be, the bound alone decides.
No kernel may reach another device: no remote copies, remote signals or barrier semaphores. Data moves between devices by JAX's collectives and lax.ppermute only.
A program may use at most 128 MiB of HBM per device.

v0:
```python
import jax
import jax.numpy as jnp
from jax import lax
from jax.sharding import PartitionSpec as P


def broadcast(block, axis, owner):
    block = jnp.where(lax.axis_index(axis) == owner, block, jnp.zeros_like(block))
    return lax.psum(block, axis)


def solve_panel(diag_block, column):
    lower = jnp.linalg.cholesky(0.5 * (diag_block + diag_block.T))
    flat = column.reshape(-1, diag_block.shape[0])
    solved = jax.scipy.linalg.solve_triangular(lower, flat.T, lower=True)
    return solved.T.reshape(column.shape)


def shards(iface_tiles, interior_sizes, coupling, factor_inverse, interface_block):
    rows_grid = lax.axis_size("prow")
    cols_grid = lax.axis_size("pcol")
    prow_index = lax.axis_index("prow")
    pcol_index = lax.axis_index("pcol")
    self_index = prow_index * cols_grid + pcol_index
    domains = iface_tiles.shape[0]
    tile_count = iface_tiles.shape[1]
    tile_width = interface_block.shape[-1]
    local_rows = interface_block.shape[1]
    local_cols = interface_block.shape[3]
    rows_per = tile_count // rows_grid
    cols_per = tile_count // cols_grid
    share_rows = tile_width // cols_grid
    live_count = interior_sizes[0]
    own_coupling = coupling[0]
    own_factor = factor_inverse[0]
    interior = own_coupling.shape[0]
    interior_live = (lax.iota(jnp.int32, interior) < live_count)[:, None]
    masked = jnp.where(interior_live, own_coupling, 0.0)
    own_tiles = lax.dynamic_index_in_dim(iface_tiles, self_index, 0, keepdims=False)
    row_order = jnp.argsort(own_tiles % rows_grid, stable=True)
    col_order = jnp.argsort(own_tiles % cols_grid, stable=True)
    weighted = jnp.dot(
        own_factor, masked, precision=lax.Precision.HIGHEST, preferred_element_type=jnp.float32
    )
    weighted = jnp.where(interior_live, weighted, 0.0).reshape(interior, tile_count, tile_width)
    row_part = jnp.take(weighted, row_order, axis=1).reshape(
        interior, rows_grid, rows_per, tile_width
    )
    col_part = jnp.take(weighted, col_order, axis=1).reshape(
        interior, cols_grid, cols_per, tile_width
    )
    contribution = -jnp.einsum(
        "kprt,kqcu->pqrctu", row_part, col_part, precision=lax.Precision.HIGHEST
    )
    received = lax.all_to_all(
        contribution.reshape(rows_grid * cols_grid, rows_per, cols_per, tile_width, tile_width),
        ("prow", "pcol"),
        split_axis=0,
        concat_axis=0,
        tiled=True,
    )
    sorted_rows = jnp.take_along_axis(
        iface_tiles, jnp.argsort(iface_tiles % rows_grid, axis=1, stable=True), axis=1
    )
    sorted_rows = sorted_rows.reshape(domains, rows_grid, rows_per)
    sorted_cols = jnp.take_along_axis(
        iface_tiles, jnp.argsort(iface_tiles % cols_grid, axis=1, stable=True), axis=1
    )
    sorted_cols = sorted_cols.reshape(domains, cols_grid, cols_per)
    target_rows = lax.dynamic_index_in_dim(sorted_rows, prow_index, 1, keepdims=False) // rows_grid
    target_cols = lax.dynamic_index_in_dim(sorted_cols, pcol_index, 1, keepdims=False) // cols_grid
    slot_ids = (target_rows[:, :, None] * local_cols + target_cols[:, None, :]).reshape(-1)
    base_tiles = interface_block.reshape(local_rows * local_cols, tile_width, tile_width)
    summed = base_tiles.at[slot_ids].add(received.reshape(-1, tile_width, tile_width))
    schur = summed.reshape(interface_block.shape)
    column = summed.reshape(local_rows, local_cols, tile_width, tile_width)[:, 0]
    diag_block = broadcast(column[0], "prow", 0)
    factored = solve_panel(diag_block, column)
    panel = broadcast(factored, "pcol", 0)
    own_share = lax.dynamic_slice_in_dim(panel, pcol_index * share_rows, share_rows, 1)
    return (schur, own_share[None])


def solution(mesh):
    in_specs = (
        P(),
        P(("prow", "pcol")),
        P(("prow", "pcol"), None, None),
        P(("prow", "pcol"), None, None),
        P("prow", None, "pcol", None, None, None),
    )
    out_specs = (P("prow", None, "pcol", None, None, None), P("prow", None, "pcol", None))
    return jax.shard_map(shards, mesh=mesh, in_specs=in_specs, out_specs=out_specs, check_vma=False)
```

profile of v0, /device:TPU:0, one launch (start us, length us, event | category | flops | bytes accessed | tf_op | source)
XLA Modules:
  0.0 673.3 jit_solution(10466884502546801936)
XLA Ops:
  7.2 8.0 %copy.40 = f32[1,8,1,16,128,128]{5,4,3,2,1,0:T(8,128)} copy(f32[1,8,1,16,128,128]{5,4,3,2,1,0:T(8,128)} %param.13) | data formatting | bytes 16777216
  15.4 1.2 sort.64
  16.6 1.2 sort.65
  18.6 16.4 %fusion.3 = f32[2048,512]{1,0:T(8,128)} fusion(f32[1,512,2048]{2,1,0:T(8,128)} %param.11, pred[512]{0:T(512)(128)(4,1)S(1)} %iota_compare_fusion.2, f32[1,512,512]{2,1,0:T(8,128)S(1)} %copy-done), kind=kOutput, calls=%fused_computation.9 | convolution fusion | flops 6444548096 | bytes 9437696 | tf_op jit(solution)/shard_map/dot_general | solution.py:42
  35.0 5.0 gather_fusion.2
  40.0 5.0 gather_fusion.3
  44.9 2.9 broadcast_select_fusion.1
  49.0 30.0 %negate_bitcast_fusion = f32[8,4,2,4,128,128]{4,5,2,0,3,1:T(8,128)} fusion(f32[512,4,4,128,1,1]{0,3,5,4,2,1:T(8,128)S(1)} %bitcast.89, f32[512,8,2,128,1,1]{0,3,2,1,5,4:T(8,128)S(1)} %bitcast.90), kind=kOutput, calls=%fused_computation.5 | convolution fusion | flops 25773998080 | bytes 25165824 | tf_op jit(solution)/shard_map/kprt,kqcu->pqrctu/dot_general | solution.py:52
  79.0 17.4 %copy.23 = f32[8,4,2,4,128,128]{5,4,3,2,1,0:T(8,128)} copy(f32[8,4,2,4,128,128]{4,5,2,0,3,1:T(8,128)} %negate_bitcast_fusion) | data formatting | bytes 33554432 | tf_op jit(solution)/shard_map/neg | solution.py:52
  96.4 7.5 %all-to-all-start = ((f32[32,2,4,128,128]{4,3,2,1,0:T(8,128)}), f32[32,2,4,128,128]{4,3,2,1,0:T(8,128)}, u32[]{:S(2)}, u32[]{:S(2)}) async-start(f32[32,2,4,128,128]{4,3,2,1,0:T(8,128)} %bitcast.86), calls=%async_computation | async-start | bytes 33554432 | tf_op jit(solution)/shard_map/all_to_all | solution.py:55
  104.8 3.9 gather_fusion.1
  109.9 3.9 gather_fusion
  114.3 362.2 %all-to-all-done = f32[32,2,4,128,128]{4,3,2,1,0:T(8,128)} async-done(((f32[32,2,4,128,128]{4,3,2,1,0:T(8,128)}), f32[32,2,4,128,128]{4,3,2,1,0:T(8,128)}, u32[]{:S(2)}, u32[]{:S(2)}) %all-to-all-start) | async-done | bytes 16777248 | tf_op jit(solution)/shard_map/all_to_all | solution.py:55
  476.4 51.3 %scatter_fusion = f32[128,128,128]{2,1,0:T(8,128)} fusion(f32[128,128,128]{2,1,0:T(8,128)} %bitcast.84, s32[256]{0:T(256)S(1)} %bitcast.95, f32[256,128,128]{2,1,0:T(8,128)} %bitcast.24), kind=kCustom, calls=%fused_computation.4 | custom fusion | flops 4194304 | bytes 50332672 | tf_op jit(solution)/shard_map/scatter-add | solution.py:74
  527.8 9.1 %copy.24 = f32[128,128,128]{1,2,0:T(8,128)} copy(f32[128,128,128]{2,1,0:T(8,128)} %scatter_fusion) | data formatting | bytes 16777216 | tf_op jit(solution)/shard_map/scatter-add | solution.py:74
  536.9 1.5 fusion.10
  538.6 65.0 %all-reduce.3.cloned.1.call-done = f32[128,128]{0,1:T(8,128)} async-done(((f32[128,128]{0,1:T(8,128)}), f32[128,128]{0,1:T(8,128)}) %all-reduce.3.cloned.1.call-update) | async-done | bytes 65552 | tf_op jit(solution)/shard_map/psum | solution.py:9
  603.7 0.9 copy.25
  604.6 0.9 fusion.13
  605.6 11.7 %cholesky.15 = f32[128,128]{1,0:T(8,128)S(1)} custom-call(f32[128,128]{1,0:T(8,128)S(1)} %fusion.12), custom_call_target="Cholesky" | custom-call | tf_op jit(solution)/shard_map/jit(cholesky)/cholesky | solution.py:13
  618.6 9.8 %custom-call.7 = f32[1,128,128]{1,2,0:T(8,128)S(1)} custom-call(f32[1,128,128]{2,1,0:T(8,128)S(1)} %fusion.9), custom_call_target="InvertDiagBlocksLowerTriangular" | custom-call | tf_op jit(solution)/shard_map/jit(_solve_triangular)/triangular_solve | solution.py:15
  628.4 2.9 convolution_select_fusion
  631.4 33.5 %all-reduce.5.cloned.1.call-done = f32[8,128,128]{2,1,0:T(8,128)} async-done(((f32[8,128,128]{2,1,0:T(8,128)}), f32[8,128,128]{2,1,0:T(8,128)}) %all-reduce.5.cloned.1.call-update) | async-done | bytes 524304 | tf_op jit(solution)/shard_map/psum | solution.py:9
  664.9 1.6 dynamic-slice_bitcast_fusion
  (51 shorter events, 5.6 us)
Async XLA Ops:
  7.2 11.4 %copy-start = (f32[1,512,512]{2,1,0:T(8,128)S(1)}, f32[1,512,512]{2,1,0:T(8,128)}, u32[]{:S(2)}) copy-start(f32[1,512,512]{2,1,0:T(8,128)} %param.12) | copy-start | bytes 3145732
  7.2 8.0 %copy-start.2 = (s32[32,16]{0,1:T(8,128)S(1)}, s32[32,16]{0,1:T(8,128)}, u32[]{:S(2)}) copy-start(s32[32,16]{0,1:T(8,128)} %param.9) | copy-start | bytes 6148
  44.9 3.4 copy-start.3
  96.4 380.1 %all-to-all-start = ((f32[32,2,4,128,128]{4,3,2,1,0:T(8,128)}), f32[32,2,4,128,128]{4,3,2,1,0:T(8,128)}, u32[]{:S(2)}, u32[]{:S(2)}) async-start(f32[32,2,4,128,128]{4,3,2,1,0:T(8,128)} %bitcast.86), calls=%async_computation | async-start | bytes 33554432 | tf_op jit(solution)/shard_map/all_to_all | solution.py:55
  103.9 499.8 %all-reduce.3.cloned.1.call-start = ((), (), s32[]{:S(2)}) async-start(), calls=%async_computation.1 | async-start | bytes 131072 | tf_op jit(solution)/shard_map/psum | solution.py:9
  527.8 138.6 %copy-start.1 = (f32[1,512,512]{2,1,0:T(8,128)S(1)}, f32[1,512,512]{2,1,0:T(8,128)}, u32[]{:S(2)}) copy-start(f32[1,512,512]{2,1,0:T(8,128)} %param.12) | copy-start | bytes 3145732
  538.4 126.5 %all-reduce.5.cloned.1.call-start = ((), (), s32[]{:S(2)}) async-start(), calls=%async_computation.2 | async-start | bytes 1048576 | tf_op jit(solution)/shard_map/psum | solution.py:9
Sparse Core Ops, SparseCore 0:
  538.5 65.1 all-reduce.2
  631.5 33.3 all-reduce.4
where the time goes:
time: 675 us; the launch traced here: 673 us
  waiting for transfers between devices  461 us (68%)
  other arithmetic  84.2 us (12%)
  local copies, waits for them, and re-layouts  56.4 us (8%)
  matrix products  49.3 us (7%)
  between operations  14.9 us (2%)
  starting transfers between devices  7.76 us (1%)
    all_to_all x1, waiting for transfers between devices, shards(): lax.all_to_all(contribution.reshape(rows_grid * cols_grid, rows_per, cols...  362 us
    psum x2, waiting for transfers between devices, broadcast(): return lax.psum(block, axis)  98.5 us
    scatter-add x1, other arithmetic, shards(): base_tiles.at[slot_ids].add(received.reshape(-1, tile_width, tile_width))  51.3 us
    dot_general x1, matrix products, shards(): jnp.einsum('kprt,kqcu->pqrctu', row_part, col_part, precision=lax.Precisi...  30 us
    neg x1, local copies, waits for them, and re-layouts, shards(): -jnp.einsum('kprt,kqcu->pqrctu', row_part, col_part, precision=lax.Precis...  17.4 us
    dot_general x1, matrix products, shards(): jnp.dot(own_factor, masked, precision=lax.Precision.HIGHEST, preferred_el...  16.4 us
  transfers between devices with their start and end apart: 3, of which 3 were waited for; matrix products, arithmetic and copies ran while one was open for 2% of the time, Pallas kernels for 0%

commit v1 on v0

v1 whole, which is shorter than its diff:
```python
import functools

import jax
import jax.numpy as jnp
from jax import lax
from jax.experimental import pallas as pl
from jax.experimental.pallas import tpu as pltpu
from jax.sharding import PartitionSpec as P


def halves(x):
    high = x.astype(jnp.bfloat16)
    low = (x - high.astype(jnp.float32)).astype(jnp.bfloat16)
    return high, low


def left_stack(x):
    high, low = halves(x)
    return jnp.concatenate([high, high, low], axis=1)


def right_stack(x):
    high, low = halves(x)
    return jnp.concatenate([high, low, high], axis=0)


def weigh_body(order_ref, live_ref, factor_ref, first_ref, second_ref, out_ref, factor_scratch):
    @pl.when(pl.program_id(0) == 0)
    def _():
        factor_scratch[...] = left_stack(factor_ref[...])

    block = jnp.concatenate([first_ref[...], second_ref[...]], axis=1)
    live = lax.broadcasted_iota(jnp.int32, block.shape, 0) < live_ref[0]
    block = jnp.where(live, block, 0.0)
    product = jnp.dot(factor_scratch[...], right_stack(block), preferred_element_type=jnp.float32)
    out_ref[...] = jnp.where(live, product, 0.0)


def weigh(order, live_count, factor, coupling, width):
    interior, iface = coupling.shape
    grid_spec = pltpu.PrefetchScalarGridSpec(
        num_scalar_prefetch=2,
        grid=(iface // (2 * width),),
        in_specs=[
            pl.BlockSpec((interior, interior), lambda i, order, live: (0, 0)),
            pl.BlockSpec((interior, width), lambda i, order, live: (0, order[2 * i])),
            pl.BlockSpec((interior, width), lambda i, order, live: (0, order[2 * i + 1])),
        ],
        out_specs=pl.BlockSpec((interior, 2 * width), lambda i, order, live: (0, i)),
        scratch_shapes=[pltpu.VMEM((interior, 3 * interior), jnp.bfloat16)],
    )
    return pl.pallas_call(
        weigh_body,
        grid_spec=grid_spec,
        out_shape=jax.ShapeDtypeStruct((interior, iface), jnp.float32),
        compiler_params=pltpu.CompilerParams(dimension_semantics=("arbitrary",)),
        name="weigh",
    )(order, live_count, factor, coupling, coupling)


def gram_body(left_ref, right_ref, out_ref, right_scratch, *, columns, width, rows_per):
    @pl.when(pl.program_id(0) == 0)
    def _():
        right_scratch[...] = right_stack(right_ref[...])

    left = left_stack(left_ref[...].T)
    for q, positions in enumerate(columns):
        for c, position in enumerate(positions):
            if position % 2:
                continue
            pair = jnp.dot(
                left,
                right_scratch[:, position * width : (position + 2) * width],
                preferred_element_type=jnp.float32,
            )
            for half in range(2):
                qq, cc = owner_of(columns, position + half)
                for r in range(rows_per):
                    out_ref[0, qq, r, cc] = pair[
                        r * width : (r + 1) * width, half * width : (half + 1) * width
                    ]


def owner_of(columns, position):
    for q, positions in enumerate(columns):
        if position in positions:
            return q, positions.index(position)


def gram(weighted, columns, rows_grid, rows_per, width):
    interior, iface = weighted.shape
    block = (len(columns), rows_per, len(columns[0]), width, width)
    return pl.pallas_call(
        functools.partial(gram_body, columns=columns, width=width, rows_per=rows_per),
        grid=(rows_grid,),
        in_specs=[
            pl.BlockSpec((interior, rows_per * width), lambda i: (0, i)),
            pl.BlockSpec((interior, iface), lambda i: (0, 0)),
        ],
        out_specs=pl.BlockSpec((1,) + block, lambda i: (i, 0, 0, 0, 0, 0)),
        out_shape=jax.ShapeDtypeStruct((rows_grid,) + block, jnp.float32),
        scratch_shapes=[pltpu.VMEM((3 * interior, iface), jnp.bfloat16)],
        compiler_params=pltpu.CompilerParams(dimension_semantics=("arbitrary",)),
        name="gram",
    )(weighted, weighted)


def assemble_body(entry_ref, first_ref, target_ref, base_ref, *refs, depth, cols_per):
    out_ref = refs[depth]
    row = pl.program_id(0)
    out_ref[...] = base_ref[...]
    for k in range(depth):
        first = first_ref[row * depth + k]
        for c in range(cols_per):
            target = target_ref[first + c]
            out_ref[0, target] = out_ref[0, target] - refs[k][0, c]


def assemble(entries, firsts, targets, base, received, depth):
    local_rows, local_cols, width, _ = base.shape
    cols_per = received.shape[1]

    def pick(k):
        return lambda i, entry, first, target: (entry[i * depth + k], 0, 0, 0)

    whole = pl.BlockSpec(
        (1, local_cols, width, width), lambda i, entry, first, target: (i, 0, 0, 0)
    )
    grid_spec = pltpu.PrefetchScalarGridSpec(
        num_scalar_prefetch=3,
        grid=(local_rows,),
        in_specs=[whole]
        + [pl.BlockSpec((1, cols_per, width, width), pick(k)) for k in range(depth)],
        out_specs=whole,
    )
    return pl.pallas_call(
        functools.partial(assemble_body, depth=depth, cols_per=cols_per),
        grid_spec=grid_spec,
        out_shape=jax.ShapeDtypeStruct(base.shape, jnp.float32),
        compiler_params=pltpu.CompilerParams(dimension_semantics=("arbitrary",)),
        name="assemble",
    )(entries, firsts, targets, base, *([received] * depth))


def ranks(keys):
    size = keys.shape[-1]
    full = keys * size + lax.iota(jnp.int32, size)
    return jnp.sum((full[..., None, :] < full[..., :, None]).astype(jnp.int32), axis=-1)


def place(rank, values):
    size = rank.shape[-1]
    hit = rank[..., None, :] == lax.iota(jnp.int32, size)[:, None]
    return jnp.sum(jnp.where(hit, values[..., None, :], 0), axis=-1)


def shards(iface_tiles, interior_sizes, coupling, factor_inverse, interface_block):
    rows_grid = lax.axis_size("prow")
    cols_grid = lax.axis_size("pcol")
    prow_index = lax.axis_index("prow")
    pcol_index = lax.axis_index("pcol")
    self_index = prow_index * cols_grid + pcol_index
    domains, tile_count = iface_tiles.shape
    width = interface_block.shape[-1]
    local_rows = interface_block.shape[1]
    local_cols = interface_block.shape[3]
    rows_per = tile_count // rows_grid
    cols_per = tile_count // cols_grid
    depth = domains * rows_per // local_rows
    columns = [
        [r * rows_per + j for r in range(q, rows_grid, cols_grid) for j in range(rows_per)]
        for q in range(cols_grid)
    ]
    rank = ranks(iface_tiles % rows_grid)
    ordered = place(rank, iface_tiles)
    origin = place(rank, jnp.broadcast_to(lax.iota(jnp.int32, tile_count), rank.shape))
    own_order = lax.dynamic_index_in_dim(origin, self_index, 0, keepdims=False)
    own_tiles = lax.dynamic_index_in_dim(ordered, self_index, 0, keepdims=False)

    weighted = weigh(own_order, interior_sizes, factor_inverse[0], coupling[0], width)

    base = interface_block.reshape(local_rows, local_cols, width, width)
    by_row = ordered.reshape(domains, rows_grid, rows_per)
    target_rows = lax.dynamic_index_in_dim(by_row, prow_index, 1, keepdims=False) // rows_grid
    by_col = ordered.reshape(domains, rows_grid // cols_grid, cols_grid, rows_per)
    target_cols = lax.dynamic_index_in_dim(by_col, pcol_index, 2, keepdims=False) // cols_grid

    zero_hits = own_tiles[:rows_per] == 0
    lead = weighted[:, : rows_per * width].reshape(-1, rows_per, width)
    lead = jnp.sum(jnp.where(zero_hits[None, :, None], lead, 0.0), axis=1)
    early = lax.dot_general(
        weighted, lead, (((0,), (0,)), ((), ())), precision=lax.Precision.HIGHEST
    ).reshape(rows_grid, rows_per, width, width)
    early_diag = jnp.sum(
        jnp.where(zero_hits[:, None, None], early[0], 0.0), axis=0
    )
    diag_base = jnp.where(self_index == 0, base[0, 0], 0.0)
    diag_block = lax.psum(diag_base - early_diag, ("prow", "pcol"))
    early = lax.all_to_all(early, "prow", split_axis=0, concat_axis=0, tiled=True)
    early = early.reshape(rows_grid * rows_per, width, width)
    early_rows = target_rows.reshape(rows_grid, cols_grid, rows_per)
    early_rows = lax.dynamic_index_in_dim(early_rows, pcol_index, 1, keepdims=False).reshape(-1)
    hit = early_rows[None, :] == lax.iota(jnp.int32, local_rows)[:, None]
    column = jnp.where(pcol_index == 0, base[:, 0], 0.0) - jnp.sum(
        jnp.where(hit[:, :, None, None], early[None], 0.0), axis=1
    )
    column = lax.psum_scatter(column, "pcol", scatter_dimension=1, tiled=True)
    lower = jnp.linalg.cholesky(0.5 * (diag_block + diag_block.T))
    flat = column.reshape(-1, width)
    panel = jax.scipy.linalg.solve_triangular(lower, flat.T, lower=True).T.reshape(column.shape)

    contribution = gram(weighted, columns, rows_grid, rows_per, width)
    received = lax.all_to_all(
        contribution.reshape(domains, rows_per, cols_per, width, width),
        ("prow", "pcol"),
        split_axis=0,
        concat_axis=0,
        tiled=True,
    )
    flat_rows = target_rows.reshape(-1)
    entries = place(ranks(flat_rows), lax.iota(jnp.int32, flat_rows.shape[0]))
    firsts = entries // rows_per * cols_per
    schur = assemble(
        entries,
        firsts,
        target_cols.reshape(-1),
        base,
        received.reshape(domains * rows_per, cols_per, width, width),
        depth,
    )
    return (schur.reshape(interface_block.shape), panel[None])


def solution(mesh):
    in_specs = (
        P(),
        P(("prow", "pcol")),
        P(("prow", "pcol"), None, None),
        P(("prow", "pcol"), None, None),
        P("prow", None, "pcol", None, None, None),
    )
    out_specs = (P("prow", None, "pcol", None, None, None), P("prow", None, "pcol", None))
    return jax.shard_map(shards, mesh=mesh, in_specs=in_specs, out_specs=out_specs, check_vma=False)
```

time: 675 us -> 466 us (0.69)
  waiting for transfers between devices: 461 us -> 336 us
  other arithmetic: 84.2 us -> 31.4 us
  Pallas kernels: 0 us -> 43.1 us
  local copies, waits for them, and re-layouts: 56.4 us -> 15.2 us
  matrix products: 49.3 us -> 11.7 us
    all_to_all x1 -> x2, waiting for transfers between devices: 362 us -> 50.3 us  [the longest x1 43.7 us: shards(): lax.all_to_all(contribution.reshape(domains, rows_per, cols_per, width, w...]
    psum x2 -> x1, waiting for transfers between devices: 98.5 us -> 286 us  [shards(): diag_block = lax.psum(diag_base - early_diag, ('prow', 'pcol'))]
    scatter-add x1 -> x0, other arithmetic: 51.3 us -> none  [shards(): base_tiles.at[slot_ids].add(received.reshape(-1, tile_width, tile_width))]
    pallas_call x0 -> x3, Pallas kernels: none -> 43.1 us  [the longest x1 19.2 us: gram(): pl.pallas_call(functools.partial(gram_body, columns=columns, width=width,...]
    dot_general x2 -> x1, matrix products: 46.4 us -> 9.87 us  [shards(): lax.dot_general(weighted, lead, (((0,), (0,)), ((), ())), precision=lax.P...]
    gather x12 -> x0, local copies, waits for them, and re-layouts: 18.3 us -> none  [the longest x1 4.98 us: shards(): jnp.take(weighted, row_order, axis=1)]
    neg x1 -> x0, local copies, waits for them, and re-layouts: 17.4 us -> none  [shards(): -jnp.einsum('kprt,kqcu->pqrctu', row_part, col_part, precision=lax.Precis...]
    scatter-add x1 -> x0, local copies, waits for them, and re-layouts: 9.09 us -> none  [shards(): base_tiles.at[slot_ids].add(received.reshape(-1, tile_width, tile_width))]
  transfers between devices with their start and end apart: 3 -> 4, of which waited for: 3 -> 3; matrix products, arithmetic and copies ran while one was open for 2% -> 9% of each run, Pallas kernels for 0% -> 4%
where the time goes in v1:
time: 466 us; the launch traced here: 465 us
  waiting for transfers between devices  336 us (72%)
  Pallas kernels  43.1 us (9%)
  other arithmetic  31.4 us (7%)
  between operations  16.3 us (3%)
  local copies, waits for them, and re-layouts  15.2 us (3%)
  matrix products  11.7 us (3%)
  starting transfers between devices  11.5 us (2%)
    psum x1, waiting for transfers between devices, shards(): diag_block = lax.psum(diag_base - early_diag, ('prow', 'pcol'))  286 us
    all_to_all x1, waiting for transfers between devices, shards(): lax.all_to_all(contribution.reshape(domains, rows_per, cols_per, width, w...  43.7 us
    pallas_call x1, Pallas kernels, gram(): pl.pallas_call(functools.partial(gram_body, columns=columns, width=width,...  19.2 us
    pallas_call x1, Pallas kernels, assemble(): pl.pallas_call(functools.partial(assemble_body, depth=depth, cols_per=col...  13.8 us
    another operation x3, other arithmetic, shards(): lower = jnp.linalg.cholesky(0.5 * (diag_block + diag_block.T))  12.4 us
    another operation x2, other arithmetic, shards(): jax.scipy.linalg.solve_triangular(lower, flat.T, lower=True)  10.5 us
    pallas_call x1, Pallas kernels, weigh(): pl.pallas_call(weigh_body, grid_spec=grid_spec, out_shape=jax.ShapeDtypeS...  10 us
    dot_general x1, matrix products, shards(): lax.dot_general(weighted, lead, (((0,), (0,)), ((), ())), precision=lax.P...  9.87 us
  transfers between devices with their start and end apart: 4, of which 3 were waited for; matrix products, arithmetic and copies ran while one was open for 9% of the time, Pallas kernels for 4%

profile of v1, /device:TPU:0, one launch (start us, length us, event | category | flops | bytes accessed | tf_op | source)
XLA Modules:
  0.0 465.4 jit_solution(8017751492840645474)
XLA Ops:
  8.7 0.7 fusion.11
  9.4 0.8 select_reduce_fusion.3
  11.1 10.0 %weigh.1.left_ref.right_ref = f32[512,2048]{1,0:T(8,128)} custom-call(s32[16]{0:T(128)} %dynamic-slice_reduce_fusion.order_ref, s32[1]{0:T(128)S(6)} %copy.81.live_ref, f32[512,512]{1,0:T(8,128)} %bitcast.57, f32[512,2048]{1,0:T(8,128)} %bitcast.51, f32[512,2048]{1,0:T(8,128)} %bitcast.52), custom_call_target="tpu_custom_call" | custom-call | tf_op jit(solution)/shard_map/weigh/pallas_call | solution.py:52
  21.1 1.1 slice.35
  22.4 0.8 select_reduce_fusion.1
  23.2 9.9 %fusion.16 = f32[2048,128]{1,0:T(8,128)} fusion(f32[512,2048]{1,0:T(8,128)} %weigh.1.left_ref.right_ref, f32[512,128]{1,0:T(8,128)S(1)} %select_reduce_fusion.1), kind=kOutput, calls=%fused_computation.64 | convolution fusion | flops 1610612736 | bytes 5505024 | tf_op jit(solution)/shard_map/dot_general | solution.py:191
  33.1 7.3 %all-to-all-start.1 = ((f32[8,2,128,128]{3,2,1,0:T(8,128)}), f32[8,2,128,128]{3,2,1,0:T(8,128)S(1)}, u32[]{:S(2)}, u32[]{:S(2)}) async-start(f32[8,2,128,128]{3,2,1,0:T(8,128)} %bitcast.11), calls=%async_computation.1 | async-start | bytes 2097152 | tf_op jit(solution)/shard_map/all_to_all | solution.py:199
  40.4 19.2 %gram.1 = f32[8,4,2,4,128,128]{5,4,3,2,1,0:T(8,128)} custom-call(f32[512,2048]{1,0:T(8,128)} %weigh.1.left_ref.right_ref, f32[512,2048]{1,0:T(8,128)} %weigh.1.left_ref.right_ref), custom_call_target="tpu_custom_call" | custom-call | tf_op jit(solution)/shard_map/gram/pallas_call | solution.py:93
  59.6 6.5 %all-to-all-done.1 = f32[8,2,128,128]{3,2,1,0:T(8,128)S(1)} async-done(((f32[8,2,128,128]{3,2,1,0:T(8,128)}), f32[8,2,128,128]{3,2,1,0:T(8,128)S(1)}, u32[]{:S(2)}, u32[]{:S(2)}) %all-to-all-start.1) | async-done | bytes 1048608 | tf_op jit(solution)/shard_map/all_to_all | solution.py:199
  66.2 3.9 all-to-all-start
  70.3 0.9 slice.37
  71.4 9.1 %copy.64 = f32[1,8,1,16,128,128]{4,5,3,1,2,0:T(8,128)} copy(f32[1,8,1,16,128,128]{5,4,3,2,1,0:T(8,128)} %param.9) | data formatting | bytes 16777216 | tf_op args[4]
  80.5 1.5 fusion.5
  83.8 1.1 select_reduce_fusion
  85.1 1.1 fusion.1
  86.2 1.0 copy.68
  87.8 285.9 %all-reduce.2.cloned.1.call-done = f32[128,128]{0,1:T(8,128)} async-done(((f32[128,128]{0,1:T(8,128)}), f32[128,128]{0,1:T(8,128)}) %all-reduce.2.cloned.1.call-update) | async-done | bytes 65552 | tf_op jit(solution)/shard_map/psum | solution.py:198
  373.7 0.9 copy.70
  374.6 0.9 fusion.8
  375.6 11.7 %cholesky.15 = f32[128,128]{1,0:T(8,128)S(1)} custom-call(f32[128,128]{1,0:T(8,128)S(1)} %fusion.7), custom_call_target="Cholesky" | custom-call | tf_op jit(solution)/shard_map/jit(cholesky)/cholesky | solution.py:208
  388.7 9.8 %custom-call.7 = f32[1,128,128]{1,2,0:T(8,128)S(1)} custom-call(f32[1,128,128]{2,1,0:T(8,128)S(1)} %fusion.3), custom_call_target="InvertDiagBlocksLowerTriangular" | custom-call | tf_op jit(solution)/shard_map/jit(_solve_triangular)/triangular_solve | solution.py:210
  398.5 1.8 convolution_bitcast_fusion
  400.3 43.7 %all-to-all-done = f32[32,2,4,128,128]{4,3,2,1,0:T(8,128)} async-done(((f32[32,2,4,128,128]{4,3,2,1,0:T(8,128)}), f32[32,2,4,128,128]{4,3,2,1,0:T(8,128)}, u32[]{:S(2)}, u32[]{:S(2)}) %all-to-all-start) | async-done | bytes 16777248 | tf_op jit(solution)/shard_map/all_to_all | solution.py:213
  444.1 13.8 %assemble.1 = f32[8,16,128,128]{3,2,1,0:T(8,128)} custom-call(s32[64]{0:T(128)} %copy-done, s32[64]{0:T(128)} %fusion.15.first_ref, s32[128]{0:T(128)} %and_select_fusion.target_ref, f32[8,16,128,128]{3,2,1,0:T(8,128)} %bitcast.50, f32[64,4,128,128]{3,2,1,0:T(8,128)} %bitcast.7.refs_0_.refs_1_.refs_2_.refs_3_.refs_4_.refs_5_.refs_6_.refs_7_, ...), custom_call_target="tpu_custom_call" | custom-call | tf_op jit(solution)/shard_map/assemble/pallas_call | solution.py:136
  (37 shorter events, 5.6 us)
Async XLA Ops:
  33.1 33.1 %all-to-all-start.1 = ((f32[8,2,128,128]{3,2,1,0:T(8,128)}), f32[8,2,128,128]{3,2,1,0:T(8,128)S(1)}, u32[]{:S(2)}, u32[]{:S(2)}) async-start(f32[8,2,128,128]{3,2,1,0:T(8,128)} %bitcast.11), calls=%async_computation.1 | async-start | bytes 2097152 | tf_op jit(solution)/shard_map/all_to_all | solution.py:199
  66.2 377.9 %all-to-all-start = ((f32[32,2,4,128,128]{4,3,2,1,0:T(8,128)}), f32[32,2,4,128,128]{4,3,2,1,0:T(8,128)}, u32[]{:S(2)}, u32[]{:S(2)}) async-start(f32[32,2,4,128,128]{4,3,2,1,0:T(8,128)} %bitcast.49), calls=%async_computation | async-start | bytes 33554432 | tf_op jit(solution)/shard_map/all_to_all | solution.py:213
  70.0 303.6 %all-reduce.2.cloned.1.call-start = ((), (), s32[]{:S(2)}) async-start(), calls=%async_computation.4 | async-start | bytes 131072 | tf_op jit(solution)/shard_map/psum | solution.py:198
  82.0 316.5 %reduce-scatter.2.cloned.1.call-start = ((), (), s32[]{:S(2)}) async-start(), calls=%async_computation.3 | async-start | bytes 655360 | tf_op jit(solution)/shard_map/reduce_scatter | solution.py:207
  83.3 360.8 %copy-start = (s32[64]{0:T(128)}, s32[64]{0:T(128)S(1)}, u32[]{:S(2)}) copy-start(s32[64]{0:T(128)S(1)} %select_reduce_fusion.6.entry_ref) | copy-start | bytes 772
Sparse Core Ops, SparseCore 0:
  82.1 291.4 all-reduce.1
Sparse Core Ops, SparseCore 1:
  87.3 30.0 reduce-scatter.1
